TPU v7x, 32 devices: a whole 2x2x4 slice. The times are simulated.
32 devices in a mesh: dp: 8 (over z, core), fsdp: 4 (over y, x).
Axes of the slice: x: 2, y: 2, z: 4, core: 2. Of those that a mesh axis runs over, the one named last changes fastest.
Arguments:
- layer_input_tokens: bfloat16 [32768, 768], P(('dp', 'fsdp')), may hold values from -6 to 6
- cotangent: bfloat16 [32768, 768], P(('dp', 'fsdp')), may hold values from -6 to 6
- lengths: int32 [160], P(('dp', 'fsdp')), may hold values from 33 to 512, as said below
- query_key_value_weight: float32 [768, 2304], P(('dp', 'fsdp')), may hold values from -0.21875 to 0.21875
- output_weight: float32 [768, 768], P(('dp', 'fsdp')), may hold values from -0.875 to 0.875
- up_weight: float32 [768, 3072], P(('dp', 'fsdp')), may hold values from -0.21875 to 0.21875
- down_weight: float32 [3072, 768], P(('dp', 'fsdp')), may hold values from -0.109375 to 0.109375
- a_in: float32 [768, 40], P(('dp', 'fsdp')), may hold values from -0.21875 to 0.21875
- a_down: float32 [3072, 8], P(('dp', 'fsdp')), may hold values from -0.109375 to 0.109375
- ln_gains: float32 [2, 768], P(None, ('dp', 'fsdp')), may hold values from 0.5 to 1.5
- ln_biases: float32 [2, 768], P(None, ('dp', 'fsdp')), may hold values from -3 to 3
- adapter_b: float32 [8, 6912], replicated, may hold values from -0.3 to 0.3
- moment_one: float32 [8, 6912], replicated, may hold values from -0.72 to 0.72
- moment_two: float32 [8, 6912], replicated, may hold values from 0.005 to 0.05
Outputs:
- layer_out: bfloat16 [32768, 768], P(('dp', 'fsdp'))
- input_grad: bfloat16 [32768, 768], P(('dp', 'fsdp'))
- b_grad: float32 [8, 6912], replicated
- grad_norm: float32 [], replicated
- moment_one_new: float32 [8, 6912], replicated
- moment_two_new: float32 [8, 6912], replicated
- adapter_b_new: float32 [8, 6912], replicated
Inputs may be any that keep to these rules, and one draw needn't show every extreme that they name: `lengths`: item 5 j + i lies in bucket i of its set; its length is more than half of its bucket and at most the bucket. Some item has exactly 512 valid tokens.
All inputs are finite; a program needn't handle non-finite values.
Results may differ from a plain program's by a relative error of at most 0.012.
The roundings to bfloat16 on the way count: a program that leaves them out, or rounds other values in their place, can miss the bound.
Values may be sent and summed in bfloat16 or wider, within the bound.
A program may use at most 192 MiB of HBM per device.

v0:
```python
import jax
import jax.numpy as jnp
from jax import lax
from jax.sharding import PartitionSpec as P

HEAD = 64
ITEM_LEN = 512
STEP = 10
adapter_scale = 2.0
ln_eps = 1e-05
clip_norm = 256.0
beta_one = 0.9
beta_two = 0.98
learn_rate = 0.02
decay_rate = 0.01


def bucket_plan(full):
    return (
        (0, full, 1, 0),
        (full, full // 2, 1, 1),
        (full * 3 // 2, full // 4, 1, 2),
        (full * 7 // 4, full // 8, 2, 3),
    )


def keep_mask(lengths_set, full):
    parts = []
    for offset, size, count, first in bucket_plan(full):
        positions = jnp.arange(size, dtype=jnp.int32)
        bounds = lengths_set[:, first : first + count]
        mask = (positions[None, None, :] < bounds[:, :, None]).astype(jnp.float32)
        parts.append(mask.reshape(lengths_set.shape[0], count * size))
    return jnp.concatenate(parts, axis=1)


def product_result(left, right):
    return jnp.dot(left, right, preferred_element_type=jnp.float32)


def transposed_product(left, right):
    return lax.dot_general(
        left, right, (((1,), (1,)), ((), ())), preferred_element_type=jnp.float32
    )


def product_tn(left, right):
    return lax.dot_general(
        left, right, (((0,), (0,)), ((), ())), preferred_element_type=jnp.float32
    )


def norm_forward(resid, gain, shift):
    center = resid - jnp.mean(resid, axis=1, keepdims=True)
    variance = jnp.mean(center * center, axis=1, keepdims=True)
    inv_std = lax.rsqrt(variance + ln_eps)
    normed = center * inv_std
    return (normed * gain + shift, normed, inv_std)


def norm_backward(grad_out, normed, inv_std, gain):
    scaled = grad_out * gain
    return inv_std * (
        scaled
        - jnp.mean(scaled, axis=1, keepdims=True)
        - normed * jnp.mean(scaled * normed, axis=1, keepdims=True)
    )


def gelu_exact(values):
    return 0.5 * values * (1.0 + jax.scipy.special.erf(values * 0.7071067811865476))


def gelu_slope(values):
    normal_cdf = 0.5 * (1.0 + jax.scipy.special.erf(values * 0.7071067811865476))
    density = jnp.exp(-0.5 * values * values) * 0.3989422804014327
    return normal_cdf + values * density


def masked_scores(query, key_rows, keep_block):
    scores = (
        jnp.einsum("gqhe,gkhe->ghqk", query, key_rows, preferred_element_type=jnp.float32) * 0.125
    )
    return jnp.where(keep_block[:, None, None, :] > 0.5, scores, -1e30)


def bucket_forward(query, key_rows, value_rows, keep_block):
    scores = masked_scores(query, key_rows, keep_block)
    highest = jnp.max(scores, axis=-1, keepdims=True)
    expo = jnp.exp(scores - highest)
    totals = jnp.sum(expo, axis=-1, keepdims=True)
    probs = (expo / totals).astype(jnp.bfloat16)
    context_rows = jnp.einsum(
        "ghqk,gkhe->gqhe", probs, value_rows, preferred_element_type=jnp.float32
    )
    return (context_rows.astype(jnp.bfloat16), highest + jnp.log(totals))


def bucket_backward(query, key_rows, value_rows, keep_block, log_total, grad_ctx):
    scores = masked_scores(query, key_rows, keep_block)
    probs = jnp.exp(scores - log_total)
    grad_probs = jnp.einsum(
        "gqhe,gkhe->ghqk", grad_ctx, value_rows, preferred_element_type=jnp.float32
    )
    delta = jnp.sum(probs * grad_probs, axis=-1, keepdims=True)
    grad_scores = (probs * (grad_probs - delta)).astype(jnp.bfloat16)
    grad_query = (
        jnp.einsum("ghqk,gkhe->gqhe", grad_scores, key_rows, preferred_element_type=jnp.float32)
        * 0.125
    )
    grad_key = (
        jnp.einsum("ghqk,gqhe->gkhe", grad_scores, query, preferred_element_type=jnp.float32)
        * 0.125
    )
    grad_value = jnp.einsum(
        "ghqk,gqhe->gkhe", probs.astype(jnp.bfloat16), grad_ctx, preferred_element_type=jnp.float32
    )
    return (
        grad_query.astype(jnp.bfloat16),
        grad_key.astype(jnp.bfloat16),
        grad_value.astype(jnp.bfloat16),
    )


def set_forward(operands):
    query, key_rows, value_rows, lens = operands
    heads, size_head = (query.shape[1], query.shape[2])
    keep_set = keep_mask(lens[None, :], ITEM_LEN)[0]
    contexts = []
    totals = []
    for offset, size, count, first in bucket_plan(ITEM_LEN):
        span = count * size
        shape = (count, size, heads, size_head)
        context_rows, log_total = bucket_forward(
            query[offset : offset + span].reshape(shape),
            key_rows[offset : offset + span].reshape(shape),
            value_rows[offset : offset + span].reshape(shape),
            keep_set[offset : offset + span].reshape(count, size),
        )
        contexts.append(context_rows.reshape(span, heads, size_head))
        totals.append(log_total)
    return (jnp.concatenate(contexts, axis=0), tuple(totals))


def set_backward(operands):
    query, key_rows, value_rows, lens, log_totals, grad_ctx = operands
    heads, size_head = (query.shape[1], query.shape[2])
    keep_set = keep_mask(lens[None, :], ITEM_LEN)[0]
    grads_q = []
    grads_k = []
    grads_v = []
    for index, (offset, size, count, first) in enumerate(bucket_plan(ITEM_LEN)):
        span = count * size
        shape = (count, size, heads, size_head)
        grad_q, grad_k, grad_v = bucket_backward(
            query[offset : offset + span].reshape(shape),
            key_rows[offset : offset + span].reshape(shape),
            value_rows[offset : offset + span].reshape(shape),
            keep_set[offset : offset + span].reshape(count, size),
            log_totals[index],
            grad_ctx[offset : offset + span].reshape(shape),
        )
        grads_q.append(grad_q.reshape(span, heads, size_head))
        grads_k.append(grad_k.reshape(span, heads, size_head))
        grads_v.append(grad_v.reshape(span, heads, size_head))
    return (
        jnp.concatenate(grads_q, axis=0),
        jnp.concatenate(grads_k, axis=0),
        jnp.concatenate(grads_v, axis=0),
    )


def adam_update(gradient, grad_norm, moment_old, second_old, weights):
    clipped = gradient * jnp.minimum(1.0, clip_norm / (grad_norm + 1e-06))
    moment_new = beta_one * moment_old + (1.0 - beta_one) * clipped
    second_new = beta_two * second_old + (1.0 - beta_two) * clipped * clipped
    first_hat = moment_new / (1.0 - beta_one**STEP)
    second_hat = second_new / (1.0 - beta_two**STEP)
    weights_new = weights - learn_rate * (
        first_hat / (jnp.sqrt(second_hat) + 1e-08) + decay_rate * weights
    )
    return (moment_new, second_new, weights_new)


def on_device(
    layer_input_tokens,
    cotangent,
    lengths,
    query_key_value_weight,
    output_weight,
    up_weight,
    down_weight,
    a_in,
    a_down,
    ln_gains,
    ln_biases,
    adapter_b,
    moment_one,
    moment_two,
):
    total_rows, width = layer_input_tokens.shape
    span_all = 2 * ITEM_LEN
    sets = total_rows // span_all
    lowrank = adapter_b.shape[0]
    hidden = up_weight.shape[1]
    head_count = width // HEAD
    brain_float_type = jnp.bfloat16
    gathered = (
        lax.all_gather(
            query_key_value_weight.astype(brain_float_type), ("dp", "fsdp"), axis=0, tiled=True
        ),
        lax.all_gather(output_weight.astype(brain_float_type), ("dp", "fsdp"), axis=0, tiled=True),
        lax.all_gather(up_weight.astype(brain_float_type), ("dp", "fsdp"), axis=0, tiled=True),
        lax.all_gather(down_weight.astype(brain_float_type), ("dp", "fsdp"), axis=0, tiled=True),
        lax.all_gather(a_in.astype(brain_float_type), ("dp", "fsdp"), axis=0, tiled=True),
        lax.all_gather(a_down.astype(brain_float_type), ("dp", "fsdp"), axis=0, tiled=True),
        lax.all_gather(ln_gains.astype(brain_float_type), ("dp", "fsdp"), axis=1, tiled=True),
        lax.all_gather(ln_biases.astype(brain_float_type), ("dp", "fsdp"), axis=1, tiled=True),
    )
    (
        projection_weight_gradient,
        output_weight_gradient,
        up_weight_gradient,
        down_weight_gradient,
        g_ain,
        g_adown,
        g_gain,
        g_bias,
    ) = gathered
    gain_full = g_gain.astype(jnp.float32)
    bias_full = g_bias.astype(jnp.float32)
    lengths_set = lengths.reshape(sets, 5)
    keep = keep_mask(lengths_set, ITEM_LEN)
    keep_rows = keep.reshape(-1, 1)
    b_low = adapter_b.astype(brain_float_type)
    query_adapter_matrix = b_low[:, :width]
    key_adapter_matrix = b_low[:, width : 2 * width]
    value_adapter_matrix = b_low[:, 2 * width : 3 * width]
    attention_adapter_bias = b_low[:, 3 * width : 4 * width]
    upper_adapter_matrix = b_low[:, 4 * width : 4 * width + hidden]
    lower_adapter_matrix = b_low[:, 4 * width + hidden :]
    projection_down_matrix = product_result(layer_input_tokens, g_ain[:, : 3 * lowrank]).astype(
        brain_float_type
    )
    adapter_projection_delta = jnp.concatenate(
        [
            product_result(projection_down_matrix[:, :lowrank], query_adapter_matrix),
            product_result(projection_down_matrix[:, lowrank : 2 * lowrank], key_adapter_matrix),
            product_result(projection_down_matrix[:, 2 * lowrank :], value_adapter_matrix),
        ],
        axis=1,
    )
    query_key_value = (
        product_result(layer_input_tokens, projection_weight_gradient)
        + adapter_scale * adapter_projection_delta
    ).astype(brain_float_type)
    qkv_heads = query_key_value.reshape(sets, span_all, 3, head_count, HEAD)
    query = qkv_heads[:, :, 0]
    key_rows = qkv_heads[:, :, 1]
    value_rows = qkv_heads[:, :, 2]
    context_rows, log_totals = lax.map(set_forward, (query, key_rows, value_rows, lengths_set))
    context_token_rows = context_rows.reshape(sets * span_all, width)
    attention_down_matrix = product_result(
        context_token_rows, g_ain[:, 3 * lowrank : 4 * lowrank]
    ).astype(brain_float_type)
    attention_output = product_result(
        context_token_rows, output_weight_gradient
    ) + adapter_scale * product_result(attention_down_matrix, attention_adapter_bias)
    hidden_one, normed_one, inv_one = norm_forward(
        layer_input_tokens.astype(jnp.float32) + attention_output, gain_full[0], bias_full[0]
    )
    hidden_lower_rows = hidden_one.astype(brain_float_type)
    upper_down_matrix = product_result(hidden_lower_rows, g_ain[:, 4 * lowrank :]).astype(
        brain_float_type
    )
    upper_rows = product_result(
        hidden_lower_rows, up_weight_gradient
    ) + adapter_scale * product_result(upper_down_matrix, upper_adapter_matrix)
    active_rows = gelu_exact(upper_rows).astype(brain_float_type)
    lower_down_matrix = product_result(active_rows, g_adown).astype(brain_float_type)
    feedforward_output = product_result(
        active_rows, down_weight_gradient
    ) + adapter_scale * product_result(lower_down_matrix, lower_adapter_matrix)
    output, normed_two, inv_two = norm_forward(
        hidden_one + feedforward_output, gain_full[1], bias_full[1]
    )
    layer_out = (output * keep_rows).astype(brain_float_type)
    again = (
        lax.all_gather(
            query_key_value_weight.astype(brain_float_type), ("dp", "fsdp"), axis=0, tiled=True
        ),
        lax.all_gather(output_weight.astype(brain_float_type), ("dp", "fsdp"), axis=0, tiled=True),
        lax.all_gather(up_weight.astype(brain_float_type), ("dp", "fsdp"), axis=0, tiled=True),
        lax.all_gather(down_weight.astype(brain_float_type), ("dp", "fsdp"), axis=0, tiled=True),
        lax.all_gather(a_in.astype(brain_float_type), ("dp", "fsdp"), axis=0, tiled=True),
        lax.all_gather(a_down.astype(brain_float_type), ("dp", "fsdp"), axis=0, tiled=True),
        lax.all_gather(ln_gains.astype(brain_float_type), ("dp", "fsdp"), axis=1, tiled=True),
        lax.all_gather(ln_biases.astype(brain_float_type), ("dp", "fsdp"), axis=1, tiled=True),
    )
    (
        projection_weight_gradient,
        output_weight_gradient,
        up_weight_gradient,
        down_weight_gradient,
        g_ain,
        g_adown,
        g_gain,
        g_bias,
    ) = again
    gain_full = g_gain.astype(jnp.float32)
    grad_out = cotangent.astype(jnp.float32) * keep_rows
    grad_two = norm_backward(grad_out, normed_two, inv_two, gain_full[1])
    feedforward_gradient = grad_two.astype(brain_float_type)
    lower_down_gradient = (
        adapter_scale * transposed_product(feedforward_gradient, lower_adapter_matrix)
    ).astype(brain_float_type)
    grad_active = transposed_product(
        feedforward_gradient, down_weight_gradient
    ) + transposed_product(lower_down_gradient, g_adown)
    upper_output_gradient = (grad_active * gelu_slope(upper_rows)).astype(brain_float_type)
    upper_down_gradient = (
        adapter_scale * transposed_product(upper_output_gradient, upper_adapter_matrix)
    ).astype(brain_float_type)
    grad_hidden = (
        grad_two
        + transposed_product(upper_output_gradient, up_weight_gradient)
        + transposed_product(upper_down_gradient, g_ain[:, 4 * lowrank :])
    )
    grad_one = norm_backward(grad_hidden, normed_one, inv_one, gain_full[0])
    attention_gradient = grad_one.astype(brain_float_type)
    attention_down_gradient = (
        adapter_scale * transposed_product(attention_gradient, attention_adapter_bias)
    ).astype(brain_float_type)
    grad_ctx = (
        transposed_product(attention_gradient, output_weight_gradient)
        + transposed_product(attention_down_gradient, g_ain[:, 3 * lowrank : 4 * lowrank])
    ).astype(brain_float_type)
    grad_q, grad_k, grad_v = lax.map(
        set_backward,
        (
            query,
            key_rows,
            value_rows,
            lengths_set,
            log_totals,
            grad_ctx.reshape(sets, span_all, head_count, HEAD),
        ),
    )
    grad_qkv = jnp.stack([grad_q, grad_k, grad_v], axis=2).reshape(sets * span_all, 3 * width)
    grad_uqkv = (
        adapter_scale
        * jnp.concatenate(
            [
                transposed_product(grad_qkv[:, :width], query_adapter_matrix),
                transposed_product(grad_qkv[:, width : 2 * width], key_adapter_matrix),
                transposed_product(grad_qkv[:, 2 * width :], value_adapter_matrix),
            ],
            axis=1,
        )
    ).astype(brain_float_type)
    input_grad = (
        grad_one
        + transposed_product(grad_qkv, projection_weight_gradient)
        + transposed_product(grad_uqkv, g_ain[:, : 3 * lowrank])
    ).astype(brain_float_type)
    local_gradient = adapter_scale * jnp.concatenate(
        [
            product_tn(projection_down_matrix[:, :lowrank], grad_qkv[:, :width]),
            product_tn(
                projection_down_matrix[:, lowrank : 2 * lowrank], grad_qkv[:, width : 2 * width]
            ),
            product_tn(projection_down_matrix[:, 2 * lowrank :], grad_qkv[:, 2 * width :]),
            product_tn(attention_down_matrix, attention_gradient),
            product_tn(upper_down_matrix, upper_output_gradient),
            product_tn(lower_down_matrix, feedforward_gradient),
        ],
        axis=1,
    )
    b_grad = lax.psum(local_gradient, ("dp", "fsdp"))
    grad_norm = jnp.sqrt(jnp.sum(b_grad * b_grad))
    moment_new, second_new, adapter_new = adam_update(
        b_grad, grad_norm, moment_one, moment_two, adapter_b
    )
    return (layer_out, input_grad, b_grad, grad_norm, moment_new, second_new, adapter_new)


def solution(mesh):
    placed = (
        P(("dp", "fsdp"), None),
        P(("dp", "fsdp"), None),
        P(("dp", "fsdp")),
        P(("dp", "fsdp"), None),
        P(("dp", "fsdp"), None),
        P(("dp", "fsdp"), None),
        P(("dp", "fsdp"), None),
        P(("dp", "fsdp"), None),
        P(("dp", "fsdp"), None),
        P(None, ("dp", "fsdp")),
        P(None, ("dp", "fsdp")),
        P(),
        P(),
        P(),
    )
    return jax.shard_map(
        on_device,
        mesh=mesh,
        in_specs=placed,
        out_specs=(P(("dp", "fsdp"), None), P(("dp", "fsdp"), None), P(), P(), P(), P(), P()),
        check_vma=False,
    )
```

profile of v0, /device:TPU:8, one launch (start us, length us, event | category | flops | bytes accessed | tf_op | source)
XLA Modules:
  0.0 654.7 jit_solution(7428954899423333268)
XLA Ops:
  7.2 1.7 convert_element_type.392
  10.6 1.6 convert_element_type.423
  12.3 1.6 convert_element_type.426
  22.8 57.2 %all_gather.32 = bf16[768,40]{1,0:T(8,128)(2,1)S(1)} all-gather(bf16[24,40]{1,0:T(8,128)(2,1)S(1)} %convert_element_type.393), channel_id=1, replica_groups=mesh['dp'=8,'fsdp'=4] {'dp','fsdp'}, dimensions={0}, use_global_device_ids=true | all-gather | bytes 63360 | tf_op jit(solution)/shard_map/all_gather | solution.py:215
  80.0 1.6 copy.149
  82.1 2.3 fusion.119
  84.4 2.4 fusion.122
  86.8 2.3 fusion.125
  89.9 64.0 %all-gather.1 = bf16[32,24,2]{1,2,0:T(2,128)(2,1)S(1)} all-gather(bf16[1,24,2]{1,2,0:T(2,128)(2,1)S(1)} %convert_bitcast_fusion.1), channel_id=1, replica_groups=mesh['dp'=8,'fsdp'=4] {'dp','fsdp'}, dimensions={0}, use_global_device_ids=true | all-gather | bytes 3168 | tf_op jit(solution)/shard_map/all_gather | solution.py:218
  154.0 66.0 %all-gather = bf16[32,24,2]{1,2,0:T(2,128)(2,1)S(1)} all-gather(bf16[1,24,2]{1,2,0:T(2,128)(2,1)S(1)} %convert_bitcast_fusion.2), channel_id=1, replica_groups=mesh['dp'=8,'fsdp'=4] {'dp','fsdp'}, dimensions={0}, use_global_device_ids=true | all-gather | bytes 3168 | tf_op jit(solution)/shard_map/all_gather | solution.py:217
  221.7 63.5 %all-gather.2 = bf16[32,96,8]{1,2,0:T(8,128)(2,1)S(1)} all-gather(bf16[1,96,8]{1,2,0:T(8,128)(2,1)S(1)} %convert_bitcast_fusion), channel_id=1, replica_groups=mesh['dp'=8,'fsdp'=4] {'dp','fsdp'}, dimensions={0}, use_global_device_ids=true | all-gather | bytes 50688 | tf_op jit(solution)/shard_map/all_gather | solution.py:216
  285.9 1.6 copy.167
  288.1 8.8 %fusion.9 = bf16[1024,2304]{1,0:T(8,128)(2,1)} fusion(f32[1024,768]{1,0:T(8,128)} %fusion.119, f32[1024,768]{1,0:T(8,128)} %fusion.122, f32[1024,768]{1,0:T(8,128)} %fusion.125, bf16[1024,768]{1,0:T(8,128)(2,1)S(1)} %copy-done.17, bf16[768,2304]{1,0:T(8,128)(2,1)} %all-gather.8.cloned.1.call-done), kind=kOutput, calls=%fused_computation.20 | convolution fusion | flops 3635675136 | bytes 19267584 | tf_op jit(solution)/shard_map/dot_general | solution.py:38
  297.0 6.6 %copy.153 = bf16[1024,2304]{0,1:T(8,128)(2,1)} copy(bf16[1024,2304]{1,0:T(8,128)(2,1)} %fusion.9) | data formatting | bytes 9437184 | tf_op jit(solution)/shard_map/convert_element_type | solution.py:256
  312.3 1.9 fusion.156
  314.2 5.1 fusion.157
  319.8 2.0 fusion.47
  321.8 2.0 copy-done.64
  323.7 1.8 fusion.6
  325.5 4.0 fusion.25
  330.0 2.8 fusion.99
  338.4 7.5 %fusion.162 = f32[1024,3072]{1,0:T(8,128)S(1)} fusion(bf16[1024,768]{0,1:T(8,128)(2,1)} %copy-done.8, bf16[768,3072]{1,0:T(8,128)(2,1)} %all-gather.12.cloned.1.call-done), kind=kOutput, calls=%fused_computation.253 | convolution fusion | flops 4831838208 | bytes 18874368 | tf_op jit(solution)/shard_map/dot_general | solution.py:38
  345.9 7.2 %multiply_convert_fusion.1 = (bf16[1024,3072]{1,0:T(8,128)(2,1)S(1)}, f32[1024,3072]{1,0:T(8,128)}) fusion(f32[1024,3072]{1,0:T(8,128)S(1)} %fusion.162, bf16[1024,8]{0,1:T(8,128)(2,1)S(1)} %convolution_convert_fusion.6, bf16[8,6912]{1,0:T(8,128)(2,1)S(1)} %convert_element_type.395), kind=kOutput, calls=%fused_computation.10 | convolution fusion | flops 72351744 | bytes 31522816 | tf_op jit(solution)/shard_map/dot_general | solution.py:38
  353.1 2.7 copy-done.6
  355.8 1.7 convolution_convert_fusion.5
  357.5 8.8 %fusion.163 = f32[1024,768]{0,1:T(8,128)S(1)} fusion(bf16[1024,3072]{1,0:T(8,128)(2,1)} %copy-done.6, bf16[3072,768]{1,0:T(8,128)(2,1)} %all-gather.14.cloned.1.call-done), kind=kOutput, calls=%fused_computation.254 | convolution fusion | flops 4831838208 | bytes 14155776 | tf_op jit(solution)/shard_map/dot_general | solution.py:38
  367.9 2.1 copy-done.5
  370.9 2.6 fusion.108
  373.5 8.0 %fusion.164 = f32[1024,3072]{1,0:T(8,128)} fusion(bf16[1024,768]{0,1:T(8,128)(2,1)S(1)} %get-tuple-element.118, bf16[3072,768]{1,0:T(8,128)(2,1)S(1)} %bitcast.280), kind=kOutput, calls=%fused_computation.255 | convolution fusion | flops 4831838208 | bytes 18874368 | tf_op jit(solution)/shard_map/dot_general | solution.py:42
  381.5 13.7 %fusion.5 = bf16[1024,3072]{1,0:T(8,128)(2,1)} fusion(f32[1024,3072]{1,0:T(8,128)} %get-tuple-element.136, f32[1024,3072]{1,0:T(8,128)} %fusion.164, bf16[3072,8]{0,1:T(8,128)(2,1)S(1)} %copy-done.47, bf16[1024,768]{0,1:T(8,128)(2,1)} %copy-done.18, bf16[8,6912]{1,0:T(8,128)(2,1)S(1)} %convert_element_type.395), kind=kOutput, calls=%fused_computation.6 | convolution fusion | flops 97533952 | bytes 33091584 | tf_op jit(solution)/shard_map/dot_general | solution.py:42
  395.2 10.0 %fusion.165 = f32[1024,768]{0,1:T(8,128)} fusion(bf16[1024,3072]{1,0:T(8,128)(2,1)} %fusion.5, bf16[768,3072]{1,0:T(8,128)(2,1)} %all-gather.12.cloned.1.call-done), kind=kOutput, calls=%fused_computation.256 | convolution fusion | flops 4831838208 | bytes 14155776 | tf_op jit(solution)/shard_map/dot_general | solution.py:42
  405.2 10.2 %fusion.149 = (f32[1024]{0:T(1024)S(1)}, f32[1024]{0:T(1024)S(1)}, f32[1024,768]{0,1:T(8,128)}) fusion(f32[1024]{0:T(1024)S(1)} %copy-done.53, f32[1024,768]{0,1:T(8,128)S(1)} %get-tuple-element.134, f32[1024]{0:T(1024)S(1)} %broadcast_multiply_fusion.6, f32[768]{0:T(1024)S(1)} %copy-done.62, bf16[768,40]{1,0:T(8,128)(2,1)S(1)} %all_gather.32, ...), kind=kOutput, calls=%fused_computation.243 | convolution fusion | flops 76298240 | bytes 20738048 | tf_op jit(solution)/shard_map/dot_general | solution.py:42
  415.5 2.8 fusion.84
  419.5 3.0 fusion.166
  422.5 4.4 add_convert_fusion.1
  426.9 1.8 slice.306
  428.7 1.7 fusion.152
  430.4 2.1 slice.305
  432.5 1.9 reshape.739
  434.4 1.7 fusion.54
  436.1 1.7 multiply_reduce_fusion.6
  442.8 2.0 fusion.64
  444.8 1.9 fusion.65
  448.1 1.9 multiply_reduce_fusion.1
  450.7 2.6 fusion.55
  453.3 2.2 fusion.56
  455.5 3.2 fusion.38
  458.7 7.1 %multiply_reduce_fusion = (f32[12,512]{1,0:T(8,128)S(1)}, f32[12,512,512]{1,2,0:T(8,128)}) fusion(f32[12,512,512]{1,2,0:T(8,128)S(1)} %bitcast.240, f32[12,512]{1,0:T(8,128)S(1)} %copy-done.39, bf16[512,12,64]{0,2,1:T(8,128)(2,1)S(1)} %bitcast.267, bf16[1,1024,3,12,64]{1,4,3,2,0:T(8,128)(2,1)} %bitcast.254), kind=kOutput, calls=%fused_computation.8 | convolution fusion | flops 412084224 | bytes 26787840 | tf_op jit(solution)/shard_map/while/body/eval_jaxpr/gqhe,gkhe->ghqk/dot_general | solution.py:102
  465.8 6.8 %multiply_convert_fusion = bf16[12,512,512]{1,2,0:T(8,128)(2,1)S(1)} fusion(f32[12,512,512]{1,2,0:T(8,128)} %get-tuple-element.147, f32[12,512,512]{1,2,0:T(8,128)S(1)} %bitcast.240, f32[12,512]{1,0:T(8,128)S(1)} %get-tuple-element.146, f32[12,512]{1,0:T(8,128)S(1)} %copy-done.39), kind=kLoop, calls=%fused_computation.7 | loop fusion | flops 12582912 | bytes 31506432 | tf_op jit(solution)/shard_map/while/body/eval_jaxpr/convert_element_type | solution.py:106
  472.6 4.0 fusion.43
  476.7 3.1 fusion.42
  481.0 1.9 reshape.748
  482.9 1.9 copy.176
  484.8 1.9 reshape.740
  486.7 1.9 copy.183
  488.6 1.9 reshape.744
  490.6 1.7 maximum_bitcast_fusion.2
  494.9 2.6 fusion.32
  503.4 6.9 %fusion.167 = f32[1024,768]{0,1:T(8,128)S(1)} fusion(bf16[768,2304]{1,0:T(8,128)(2,1)} %all-gather.8.cloned.1.call-done, bf16[1024,2304]{0,1:T(8,128)(2,1)} %bitcast.265), kind=kOutput, calls=%fused_computation.258 | convolution fusion | flops 3623878656 | bytes 11403264 | tf_op jit(solution)/shard_map/dot_general | solution.py:42
  510.4 2.3 add_convert_fusion
  512.7 2.7 copy.192
  517.0 123.7 %all-reduce.2.cloned.1.call-done = f32[8,6912]{1,0:T(8,128)} async-done(((f32[8,6912]{1,0:T(8,128)}), f32[8,6912]{1,0:T(8,128)}) %all-reduce.2.cloned.1.call-update) | async-done | bytes 221200 | tf_op jit(solution)/shard_map/psum | solution.py:379
  643.1 1.9 multiply_subtract_fusion
  644.9 1.6 copy.241
  (284 shorter events, 53.2 us)
Async XLA Ops:
  7.2 72.8 %copy-start.17 = (bf16[1024,768]{1,0:T(8,128)(2,1)S(1)}, bf16[1024,768]{1,0:T(8,128)(2,1)}, u32[]{:S(2)}) copy-start(bf16[1024,768]{1,0:T(8,128)(2,1)} %param.14) | copy-start | bytes 4718596
  7.2 281.0 %all-gather.8.cloned.1.call-start = ((), (), s32[]{:S(2)}) async-start(), calls=%async_computation | async-start | bytes 3649536 | tf_op jit(solution)/shard_map/all_gather | solution.py:209
  8.9 321.0 %all-gather.10.cloned.1.call-start = ((), (), s32[]{:S(2)}) async-start(), calls=%async_computation.1 | async-start | bytes 1216512 | tf_op jit(solution)/shard_map/all_gather | solution.py:212
  10.5 327.8 %all-gather.12.cloned.1.call-start = ((), (), s32[]{:S(2)}) async-start(), calls=%async_computation.2 | async-start | bytes 4866048 | tf_op jit(solution)/shard_map/all_gather | solution.py:213
  12.2 345.3 %all-gather.14.cloned.1.call-start = ((), (), s32[]{:S(2)}) async-start(), calls=%async_computation.3 | async-start | bytes 4866048 | tf_op jit(solution)/shard_map/all_gather | solution.py:214
  13.9 626.8 %all-reduce.2.cloned.1.call-start = ((), (), s32[]{:S(2)}) async-start(), calls=%async_computation.4 | async-start | bytes 442368 | tf_op jit(solution)/shard_map/psum | solution.py:379
  22.8 399.7 %copy-start.38 = (bf16[8,6912]{1,0:T(8,128)(2,1)}, bf16[8,6912]{1,0:T(8,128)(2,1)S(1)}, u32[]{:S(2)}) copy-start(bf16[8,6912]{1,0:T(8,128)(2,1)S(1)} %convert_element_type.395) | copy-start | bytes 331780
  82.1 4.7 copy-start.40
  84.4 5.4 copy-start.81
  84.4 5.4 copy-start.82
  84.4 5.5 copy-start.77
  84.4 201.5 %copy-start.26 = (bf16[1024,768]{1,0:T(8,128)(2,1)S(1)}, bf16[1024,768]{1,0:T(8,128)(2,1)}, u32[]{:S(2)}) copy-start(bf16[1024,768]{1,0:T(8,128)(2,1)} %param.15) | copy-start | bytes 4718596
  220.9 115.4 %copy-start.61 = (f32[768]{0:T(1024)}, f32[768]{0:T(1024)S(1)}, u32[]{:S(2)}) copy-start(f32[768]{0:T(1024)S(1)} %get-tuple-element.109) | copy-start | bytes 9220
  305.0 5.0 copy-start.28
  305.2 4.8 copy-start.30
  305.4 4.6 copy-start.83
  305.8 4.8 copy-start.27
  314.2 5.6 copy-start.2
  319.3 6.2 copy-start
  319.8 4.0 copy-start.64
  325.5 4.0 copy-start.56
  330.0 2.9 copy-start.58
  330.0 2.9 copy-start.20
  333.8 81.7 %copy-start.45 = (f32[1024]{0:T(1024)}, f32[1024]{0:T(1024)S(1)}, u32[]{:S(2)}) copy-start(f32[1024]{0:T(1024)S(1)} %broadcast_multiply_fusion.6) | copy-start | bytes 12292
  334.4 3.9 copy-start.52
  338.3 7.5 %copy-start.48 = (bf16[1024,8]{0,1:T(8,128)(2,1)}, bf16[1024,8]{0,1:T(8,128)(2,1)S(1)}, u32[]{:S(2)}) copy-start(bf16[1024,8]{0,1:T(8,128)(2,1)S(1)} %convolution_convert_fusion.6) | copy-start | bytes 49156
  345.9 9.9 %copy-start.47 = (bf16[3072,8]{0,1:T(8,128)(2,1)S(1)}, bf16[3072,8]{0,1:T(8,128)(2,1)}, u32[]{:S(2)}) copy-start(bf16[3072,8]{0,1:T(8,128)(2,1)} %reshape.756) | copy-start | bytes 147460
  357.5 8.9 %copy-start.50 = (bf16[1024,8]{0,1:T(8,128)(2,1)}, bf16[1024,8]{0,1:T(8,128)(2,1)S(1)}, u32[]{:S(2)}) copy-start(bf16[1024,8]{0,1:T(8,128)(2,1)S(1)} %convolution_convert_fusion.5) | copy-start | bytes 49156
  357.5 8.9 %copy-start.53 = (f32[1024]{0:T(1024)S(1)}, f32[1024]{0:T(1024)}, u32[]{:S(2)}) copy-start(f32[1024]{0:T(1024)} %copy-done.52) | copy-start | bytes 12292
  357.5 8.9 %copy-start.62 = (f32[768]{0:T(1024)S(1)}, f32[768]{0:T(1024)}, u32[]{:S(2)}) copy-start(f32[768]{0:T(1024)} %copy-done.61) | copy-start | bytes 9220
  357.5 8.9 %copy-start.69 = (f32[768]{0:T(1024)S(1)}, f32[768]{0:T(1024)}, u32[]{:S(2)}) copy-start(f32[768]{0:T(1024)} %get-tuple-element.111) | copy-start | bytes 9220
  367.4 3.5 copy-start.1
  367.9 3.0 copy-start.76
  370.0 3.5 slice-start.5
  373.5 8.0 %copy-start.18 = (bf16[1024,768]{0,1:T(8,128)(2,1)}, bf16[1024,768]{0,1:T(8,128)(2,1)S(1)}, u32[]{:S(2)}) copy-start(bf16[1024,768]{0,1:T(8,128)(2,1)S(1)} %get-tuple-element.118) | copy-start | bytes 4718596
  415.4 2.9 copy-start.70
  415.5 2.9 copy-start.72
  415.5 4.0 copy-start.80
  434.3 3.5 copy-start.14
  434.4 3.5 copy-start.42
  434.4 3.7 copy-start.31
  436.0 3.1 copy-start.29
  436.0 4.2 copy-start.12
  436.1 4.2 copy-start.55
  440.3 6.4 copy-start.3
  440.3 6.4 copy-start.22
  446.7 8.8 %slice-start = ((s8[12582912]{0:T(1024)(128)(4,1)}), s8[4194304]{0:T(1024)(128)(4,1)S(1)}, s32[]{:S(2)}) async-start(s8[12582912]{0:T(1024)(128)(4,1)} %bitcast.239), calls=%async_computation.5 | async-start | bytes 8388608
  448.1 7.4 %slice-start.1 = ((s8[12582912]{0:T(1024)(128)(4,1)}), s8[4194304]{0:T(1024)(128)(4,1)S(1)}, s32[]{:S(2)}) async-start(s8[12582912]{0:T(1024)(128)(4,1)} %bitcast.239), calls=%async_computation.6 | async-start | bytes 8388608
  450.0 5.5 slice-start.2
  450.7 4.8 copy-start.15
  450.7 4.8 copy-start.39
  479.8 10.7 %copy-start.33 = (bf16[128,12,64]{0,2,1:T(8,128)(2,1)S(1)}, bf16[128,12,64]{0,2,1:T(8,128)(2,1)}, u32[]{:S(2)}) copy-start(bf16[128,12,64]{0,2,1:T(8,128)(2,1)} %fusion.66) | copy-start | bytes 589828
  493.0 7.7 %slice-start.3 = ((s8[6291456]{0:T(1024)(128)(4,1)}), s8[2097152]{0:T(1024)(128)(4,1)S(1)}, s32[]{:S(2)}) async-start(s8[6291456]{0:T(1024)(128)(4,1)} %bitcast.257), calls=%async_computation.8 | async-start | bytes 4194304
  493.6 6.0 copy-start.7
  493.6 5.0 copy-start.41
  493.6 7.1 %slice-start.4 = ((s8[6291456]{0:T(1024)(128)(4,1)}), s8[4194304]{0:T(1024)(128)(4,1)S(1)}, s32[]{:S(2)}) async-start(s8[6291456]{0:T(1024)(128)(4,1)} %bitcast.257), calls=%async_computation.9 | async-start | bytes 8388608
  503.4 6.9 %copy-start.4 = (f32[1024,768]{0,1:T(8,128)S(1)}, f32[1024,768]{0,1:T(8,128)}, u32[]{:S(2)}) copy-start(f32[1024,768]{0,1:T(8,128)} %get-tuple-element.139) | copy-start | bytes 9437188
  503.4 6.9 %copy-start.46 = (f32[1024]{0:T(1024)S(1)}, f32[1024]{0:T(1024)}, u32[]{:S(2)}) copy-start(f32[1024]{0:T(1024)} %copy-done.45) | copy-start | bytes 12292
  503.4 6.9 %copy-start.54 = (f32[1024]{0:T(1024)S(1)}, f32[1024]{0:T(1024)}, u32[]{:S(2)}) copy-start(f32[1024]{0:T(1024)} %copy-done.52) | copy-start | bytes 12292
  503.4 6.9 %copy-start.71 = (f32[1024]{0:T(1024)S(1)}, f32[1024]{0:T(1024)}, u32[]{:S(2)}) copy-start(f32[1024]{0:T(1024)} %copy-done.70) | copy-start | bytes 12292
  503.4 6.9 %copy-start.73 = (f32[1024]{0:T(1024)S(1)}, f32[1024]{0:T(1024)}, u32[]{:S(2)}) copy-start(f32[1024]{0:T(1024)} %copy-done.72) | copy-start | bytes 12292
  512.7 130.3 %copy-start.32 = (f32[8,6912]{1,0:T(8,128)S(1)}, f32[8,6912]{1,0:T(8,128)}, u32[]{:S(2)}) copy-start(f32[8,6912]{1,0:T(8,128)} %param.25) | copy-start | bytes 663556
  512.7 130.3 %copy-start.43 = (f32[8,6912]{1,0:T(8,128)S(1)}, f32[8,6912]{1,0:T(8,128)}, u32[]{:S(2)}) copy-start(f32[8,6912]{1,0:T(8,128)} %param.27) | copy-start | bytes 663556
  512.7 130.4 %copy-start.44 = (f32[8,6912]{1,0:T(8,128)S(1)}, f32[8,6912]{1,0:T(8,128)}, u32[]{:S(2)}) copy-start(f32[8,6912]{1,0:T(8,128)} %param.26) | copy-start | bytes 663556
  (32 other events, 60.1 us)
Sparse Core Ops, SparseCore 0:
  11.4 60.8 all-gather.7
  75.2 52.5 all-gather.9
  131.3 63.4 all-gather.11
  198.1 62.1 all-gather.13
  503.5 137.1 all-reduce.1
where the time goes:
time: 659 us; the launch traced here: 655 us
  blocking collectives  251 us (38%)
  matrix products  168 us (25%)
  waiting for transfers between devices  124 us (19%)
  local copies, waits for them, and re-layouts  54 us (8%)
  other arithmetic  41 us (6%)
  between operations  17.3 us (3%)
    psum x1, waiting for transfers between devices, on_device(): b_grad = lax.psum(local_gradient, ('dp', 'fsdp'))  124 us
    all_gather x1, blocking collectives, on_device(): lax.all_gather(ln_gains.astype(brain_float_type), ('dp', 'fsdp'), axis=1,...  66 us
    all_gather x1, blocking collectives, on_device(): lax.all_gather(ln_biases.astype(brain_float_type), ('dp', 'fsdp'), axis=1...  64 us
    all_gather x1, blocking collectives, on_device(): lax.all_gather(a_down.astype(brain_float_type), ('dp', 'fsdp'), axis=0, t...  63.5 us
    dot_general x11, matrix products, transposed_product(): lax.dot_general(left, right, (((1,), (1,)), ((), ())), preferred_element_...  63.5 us
    all_gather x1, blocking collectives, on_device(): lax.all_gather(a_in.astype(brain_float_type), ('dp', 'fsdp'), axis=0, til...  57.2 us
    dot_general x14, matrix products, product_result(): return jnp.dot(left, right, preferred_element_type=jnp.float32)  47 us
    unnamed x188, local copies, waits for them, and re-layouts  22.4 us
  transfers between devices with their start and end apart: 5, of which 1 were waited for; matrix products, arithmetic and copies ran while one was open for 16% of the time, Pallas kernels for 0%

commit v1 on v0

--- a/solution.py
+++ b/solution.py
@@ -13,6 +13,18 @@
 beta_two = 0.98
 learn_rate = 0.02
 decay_rate = 0.01
+
+
+def doubled_up(value, axis, dim):
+    ways, here, step = (lax.axis_size(axis), lax.axis_index(axis), value.shape[dim])
+    line, have = (value, 1)
+    while have < ways:
+        line = jnp.concatenate(
+            [line, lax.ppermute(line, axis, [(d, (d - have) % ways) for d in range(ways)])],
+            axis=dim,
+        )
+        have = 2 * have
+    return jnp.roll(line, here * step, axis=dim)
 
 
 def bucket_plan(full):
@@ -215,7 +227,7 @@
         lax.all_gather(a_in.astype(brain_float_type), ("dp", "fsdp"), axis=0, tiled=True),
         lax.all_gather(a_down.astype(brain_float_type), ("dp", "fsdp"), axis=0, tiled=True),
         lax.all_gather(ln_gains.astype(brain_float_type), ("dp", "fsdp"), axis=1, tiled=True),
-        lax.all_gather(ln_biases.astype(brain_float_type), ("dp", "fsdp"), axis=1, tiled=True),
+        doubled_up(ln_biases.astype(brain_float_type), ("dp", "fsdp"), 1),
     )
     (
         projection_weight_gradient,

time: 659 us -> 614 us (0.932)
  blocking collectives: 251 us -> 184 us
  starting transfers between devices: 0.21 us -> 18 us
    all_gather x1 -> x0, blocking collectives: 64 us -> none  [on_device(): lax.all_gather(ln_biases.astype(brain_float_type), ('dp', 'fsdp'), axis=1...]
    ppermute x0 -> x5, starting transfers between devices: none -> 17.8 us  [doubled_up(): lax.ppermute(line, axis, [(d, (d - have) % ways) for d in range(ways)])]
  transfers between devices with their start and end apart: 5 -> 10, of which waited for: 1 -> 3; matrix products, arithmetic and copies ran while one was open for 16% -> 17% of each run, Pallas kernels for 0% -> 0%
where the time goes in v1:
time: 614 us; the launch traced here: 609 us
  blocking collectives  184 us (30%)
  matrix products  169 us (28%)
  waiting for transfers between devices  124 us (20%)
  local copies, waits for them, and re-layouts  55.2 us (9%)
  other arithmetic  42.4 us (7%)
  starting transfers between devices  18 us (3%)
  between operations  17.3 us (3%)
    psum x1, waiting for transfers between devices, on_device(): b_grad = lax.psum(local_gradient, ('dp', 'fsdp'))  123 us
    all_gather x1, blocking collectives, on_device(): lax.all_gather(ln_gains.astype(brain_float_type), ('dp', 'fsdp'), axis=1,...  64.9 us
    dot_general x11, matrix products, transposed_product(): lax.dot_general(left, right, (((1,), (1,)), ((), ())), preferred_element_...  63.5 us
    all_gather x1, blocking collectives, on_device(): lax.all_gather(a_down.astype(brain_float_type), ('dp', 'fsdp'), axis=0, t...  61.9 us
    all_gather x1, blocking collectives, on_device(): lax.all_gather(a_in.astype(brain_float_type), ('dp', 'fsdp'), axis=0, til...  56.7 us
    dot_general x14, matrix products, product_result(): return jnp.dot(left, right, preferred_element_type=jnp.float32)  48.1 us
    unnamed x188, local copies, waits for them, and re-layouts  22.6 us
    ppermute x5, starting transfers between devices, doubled_up(): lax.ppermute(line, axis, [(d, (d - have) % ways) for d in range(ways)])  17.8 us
  transfers between devices with their start and end apart: 10, of which 3 were waited for; matrix products, arithmetic and copies ran while one was open for 17% of the time, Pallas kernels for 0%

profile of v1, /device:TPU:8, one launch (start us, length us, event | category | flops | bytes accessed | tf_op | source)
XLA Modules:
  0.0 608.8 jit_solution(12405517451787973335)
XLA Ops:
  10.5 1.6 convert_element_type.423
  12.9 1.8 collective-permute-start
  20.1 56.7 %all_gather.29 = bf16[768,40]{1,0:T(8,128)(2,1)S(1)} all-gather(bf16[24,40]{1,0:T(8,128)(2,1)S(1)} %convert_element_type.393), channel_id=1, replica_groups=mesh['dp'=8,'fsdp'=4] {'dp','fsdp'}, dimensions={0}, use_global_device_ids=true | all-gather | bytes 63360 | tf_op jit(solution)/shard_map/all_gather | solution.py:227
  76.8 1.9 convolution_convert_fusion.4
  78.8 2.3 fusion.119
  81.1 2.4 fusion.122
  83.4 2.2 fusion.125
  88.5 64.9 %all-gather = bf16[32,24,2]{1,2,0:T(2,128)(2,1)S(1)} all-gather(bf16[1,24,2]{1,2,0:T(2,128)(2,1)S(1)} %convert_bitcast_fusion.1), channel_id=1, replica_groups=mesh['dp'=8,'fsdp'=4] {'dp','fsdp'}, dimensions={0}, use_global_device_ids=true | all-gather | bytes 3168 | tf_op jit(solution)/shard_map/all_gather | solution.py:229
  156.2 3.9 collective-permute-start.1
  161.5 7.2 %collective-permute-start.2 = (bf16[2,96]{1,0:T(2,128)(2,1)S(1)}, bf16[2,96]{1,0:T(2,128)(2,1)S(1)}, u32[]{:S(2)}, u32[]{:S(2)}) collective-permute-start(bf16[2,96]{1,0:T(2,128)(2,1)S(1)} %pad_maximum_fusion.6), channel_id=1, source_target_pairs={{0,28},{1,29},{2,30},{3,31},{4,0},{5,1},{6,2},{7,3},{8,4},{9,5},{1... | collective-permute-start | bytes 1160 | tf_op jit(solution)/shard_map/ppermute | solution.py:23
  170.0 3.8 collective-permute-start.3
  173.8 61.9 %all-gather.1 = bf16[32,96,8]{1,2,0:T(8,128)(2,1)} all-gather(bf16[1,96,8]{1,2,0:T(8,128)(2,1)S(1)} %convert_bitcast_fusion), channel_id=1, replica_groups=mesh['dp'=8,'fsdp'=4] {'dp','fsdp'}, dimensions={0}, use_global_device_ids=true | all-gather | bytes 50688 | tf_op jit(solution)/shard_map/all_gather | solution.py:228
  237.0 1.8 copy.147
  242.9 8.9 %fusion.9 = bf16[1024,2304]{1,0:T(8,128)(2,1)} fusion(f32[1024,768]{1,0:T(8,128)} %fusion.119, f32[1024,768]{1,0:T(8,128)} %fusion.122, f32[1024,768]{1,0:T(8,128)} %fusion.125, bf16[1024,768]{1,0:T(8,128)(2,1)S(1)} %copy-done.17, bf16[768,2304]{1,0:T(8,128)(2,1)} %all-gather.7.cloned.1.call-done), kind=kOutput, calls=%fused_computation.20 | convolution fusion | flops 3635675136 | bytes 19267584 | tf_op jit(solution)/shard_map/dot_general | solution.py:50
  251.7 6.7 %copy.151 = bf16[1024,2304]{0,1:T(8,128)(2,1)} copy(bf16[1024,2304]{1,0:T(8,128)(2,1)} %fusion.9) | data formatting | bytes 9437184 | tf_op jit(solution)/shard_map/convert_element_type | solution.py:268
  267.2 1.9 fusion.156
  269.1 5.1 fusion.157
  274.7 2.0 fusion.47
  276.7 2.0 copy-done.64
  278.7 1.8 fusion.6
  280.5 4.0 fusion.25
  285.0 2.8 fusion.99
  293.3 7.5 %fusion.162 = f32[1024,3072]{1,0:T(8,128)S(1)} fusion(bf16[1024,768]{0,1:T(8,128)(2,1)} %copy-done.8, bf16[768,3072]{1,0:T(8,128)(2,1)} %all-gather.11.cloned.1.call-done), kind=kOutput, calls=%fused_computation.256 | convolution fusion | flops 4831838208 | bytes 18874368 | tf_op jit(solution)/shard_map/dot_general | solution.py:50
  300.8 6.9 %multiply_convert_fusion.1 = (bf16[1024,3072]{1,0:T(8,128)(2,1)S(1)}, f32[1024,3072]{1,0:T(8,128)}) fusion(f32[1024,3072]{1,0:T(8,128)S(1)} %fusion.162, bf16[1024,8]{0,1:T(8,128)(2,1)S(1)} %convolution_convert_fusion.6, bf16[8,6912]{1,0:T(8,128)(2,1)S(1)} %convert_element_type.395), kind=kOutput, calls=%fused_computation.10 | convolution fusion | flops 72351744 | bytes 31522816 | tf_op jit(solution)/shard_map/dot_general | solution.py:50
  307.7 2.7 copy-done.6
  310.4 1.7 convolution_convert_fusion.5
  312.2 8.8 %fusion.163 = f32[1024,768]{0,1:T(8,128)S(1)} fusion(bf16[1024,3072]{1,0:T(8,128)(2,1)} %copy-done.6, bf16[3072,768]{1,0:T(8,128)(2,1)} %all-gather.13.cloned.1.call-done), kind=kOutput, calls=%fused_computation.257 | convolution fusion | flops 4831838208 | bytes 14155776 | tf_op jit(solution)/shard_map/dot_general | solution.py:50
  322.5 2.1 copy-done.5
  325.6 2.6 fusion.108
  328.2 8.1 %fusion.164 = f32[1024,3072]{1,0:T(8,128)} fusion(bf16[1024,768]{0,1:T(8,128)(2,1)S(1)} %get-tuple-element.118, bf16[3072,768]{1,0:T(8,128)(2,1)S(1)} %bitcast.272), kind=kOutput, calls=%fused_computation.258 | convolution fusion | flops 4831838208 | bytes 18874368 | tf_op jit(solution)/shard_map/dot_general | solution.py:54
  336.2 13.7 %fusion.5 = bf16[1024,3072]{1,0:T(8,128)(2,1)} fusion(f32[1024,3072]{1,0:T(8,128)} %get-tuple-element.136, f32[1024,3072]{1,0:T(8,128)} %fusion.164, bf16[3072,8]{0,1:T(8,128)(2,1)S(1)} %copy-done.47, bf16[1024,768]{0,1:T(8,128)(2,1)} %copy-done.18, bf16[8,6912]{1,0:T(8,128)(2,1)S(1)} %convert_element_type.395), kind=kOutput, calls=%fused_computation.6 | convolution fusion | flops 97533952 | bytes 33091584 | tf_op jit(solution)/shard_map/dot_general | solution.py:54
  349.9 10.0 %fusion.165 = f32[1024,768]{0,1:T(8,128)} fusion(bf16[1024,3072]{1,0:T(8,128)(2,1)} %fusion.5, bf16[768,3072]{1,0:T(8,128)(2,1)} %all-gather.11.cloned.1.call-done), kind=kOutput, calls=%fused_computation.259 | convolution fusion | flops 4831838208 | bytes 14155776 | tf_op jit(solution)/shard_map/dot_general | solution.py:54
  359.9 10.3 %fusion.149 = (f32[1024]{0:T(1024)S(1)}, f32[1024]{0:T(1024)S(1)}, f32[1024,768]{0,1:T(8,128)}) fusion(f32[1024]{0:T(1024)S(1)} %copy-done.53, f32[1024,768]{0,1:T(8,128)S(1)} %get-tuple-element.134, f32[1024]{0:T(1024)S(1)} %broadcast_multiply_fusion.6, f32[768]{0:T(1024)S(1)} %copy-done.62, bf16[768,40]{1,0:T(8,128)(2,1)S(1)} %all_gather.29, ...), kind=kOutput, calls=%fused_computation.246 | convolution fusion | flops 76298240 | bytes 20738048 | tf_op jit(solution)/shard_map/dot_general | solution.py:54
  370.2 2.8 fusion.84
  374.2 3.0 fusion.166
  377.2 4.4 add_convert_fusion.1
  381.5 1.8 slice.306
  383.4 1.7 fusion.152
  385.1 2.1 slice.305
  387.1 1.9 reshape.739
  389.0 1.7 fusion.54
  390.7 1.7 multiply_reduce_fusion.6
  397.5 2.0 fusion.64
  399.5 1.8 fusion.65
  402.7 1.9 multiply_reduce_fusion.1
  405.3 2.6 fusion.55
  407.9 2.1 fusion.56
  410.1 3.2 fusion.38
  413.3 7.2 %multiply_reduce_fusion = (f32[12,512]{1,0:T(8,128)S(1)}, f32[12,512,512]{1,2,0:T(8,128)}) fusion(f32[12,512,512]{1,2,0:T(8,128)S(1)} %bitcast.233, f32[12,512]{1,0:T(8,128)S(1)} %copy-done.39, bf16[512,12,64]{0,2,1:T(8,128)(2,1)S(1)} %bitcast.260, bf16[1,1024,3,12,64]{1,4,3,2,0:T(8,128)(2,1)} %bitcast.247), kind=kOutput, calls=%fused_computation.8 | convolution fusion | flops 412084224 | bytes 26787840 | tf_op jit(solution)/shard_map/while/body/eval_jaxpr/gqhe,gkhe->ghqk/dot_general | solution.py:114
  420.5 6.8 %multiply_convert_fusion = bf16[12,512,512]{1,2,0:T(8,128)(2,1)S(1)} fusion(f32[12,512,512]{1,2,0:T(8,128)} %get-tuple-element.147, f32[12,512,512]{1,2,0:T(8,128)S(1)} %bitcast.233, f32[12,512]{1,0:T(8,128)S(1)} %get-tuple-element.146, f32[12,512]{1,0:T(8,128)S(1)} %copy-done.39), kind=kLoop, calls=%fused_computation.7 | loop fusion | flops 12582912 | bytes 31506432 | tf_op jit(solution)/shard_map/while/body/eval_jaxpr/convert_element_type | solution.py:118
  427.3 4.0 fusion.43
  431.3 3.2 fusion.42
  435.6 1.9 reshape.748
  437.5 1.9 copy.172
  439.5 1.9 reshape.740
  441.4 1.9 copy.179
  443.3 1.9 reshape.744
  445.3 1.7 maximum_bitcast_fusion.2
  449.5 2.6 fusion.32
  458.1 6.9 %fusion.167 = f32[1024,768]{0,1:T(8,128)S(1)} fusion(bf16[768,2304]{1,0:T(8,128)(2,1)} %all-gather.7.cloned.1.call-done, bf16[1024,2304]{0,1:T(8,128)(2,1)} %bitcast.258), kind=kOutput, calls=%fused_computation.261 | convolution fusion | flops 3623878656 | bytes 11403264 | tf_op jit(solution)/shard_map/dot_general | solution.py:54
  465.0 2.3 add_convert_fusion
  467.4 2.7 copy.188
  471.6 123.2 %all-reduce.2.cloned.1.call-done = f32[8,6912]{1,0:T(8,128)} async-done(((f32[8,6912]{1,0:T(8,128)}), f32[8,6912]{1,0:T(8,128)}) %all-reduce.2.cloned.1.call-update) | async-done | bytes 221200 | tf_op jit(solution)/shard_map/psum | solution.py:391
  597.2 1.9 multiply_subtract_fusion
  (296 shorter events, 62.8 us)
Async XLA Ops:
  7.2 235.7 %all-gather.7.cloned.1.call-start = ((), (), s32[]{:S(2)}) async-start(), calls=%async_computation | async-start | bytes 3649536 | tf_op jit(solution)/shard_map/all_gather | solution.py:221
  8.8 276.1 %all-gather.9.cloned.1.call-start = ((), (), s32[]{:S(2)}) async-start(), calls=%async_computation.1 | async-start | bytes 1216512 | tf_op jit(solution)/shard_map/all_gather | solution.py:224
  10.4 282.9 %all-gather.11.cloned.1.call-start = ((), (), s32[]{:S(2)}) async-start(), calls=%async_computation.2 | async-start | bytes 4866048 | tf_op jit(solution)/shard_map/all_gather | solution.py:225
  12.1 300.0 %all-gather.13.cloned.1.call-start = ((), (), s32[]{:S(2)}) async-start(), calls=%async_computation.3 | async-start | bytes 4866048 | tf_op jit(solution)/shard_map/all_gather | solution.py:226
  12.9 143.2 %collective-permute-start = (bf16[2,24]{1,0:T(2,128)(2,1)S(1)}, bf16[2,24]{1,0:T(2,128)(2,1)S(1)}, u32[]{:S(2)}, u32[]{:S(2)}) collective-permute-start(bf16[2,24]{1,0:T(2,128)(2,1)S(1)} %convert_element_type.420), channel_id=1, source_target_pairs={{0,31},{1,0},{2,1},{3,2},{4,3},{5,4},{6,5},{7,6},{8,7},{9,8},{10,9... | collective-permute-start | bytes 296 | tf_op jit(solution)/shard_map/ppermute | solution.py:23
  16.3 578.6 %all-reduce.2.cloned.1.call-start = ((), (), s32[]{:S(2)}) async-start(), calls=%async_computation.4 | async-start | bytes 442368 | tf_op jit(solution)/shard_map/psum | solution.py:391
  20.1 357.1 %copy-start.38 = (bf16[8,6912]{1,0:T(8,128)(2,1)}, bf16[8,6912]{1,0:T(8,128)(2,1)S(1)}, u32[]{:S(2)}) copy-start(bf16[8,6912]{1,0:T(8,128)(2,1)S(1)} %convert_element_type.395) | copy-start | bytes 331780
  78.7 4.7 copy-start.40
  81.0 5.4 copy-start.81
  81.0 7.5 %copy-start.77 = (f32[96,8]{0,1:T(8,128)S(1)}, f32[96,8]{0,1:T(8,128)}, u32[]{:S(2)}) copy-start(f32[96,8]{0,1:T(8,128)} %param.22) | copy-start | bytes 9220
  81.1 155.9 %copy-start.17 = (bf16[1024,768]{1,0:T(8,128)(2,1)S(1)}, bf16[1024,768]{1,0:T(8,128)(2,1)}, u32[]{:S(2)}) copy-start(bf16[1024,768]{1,0:T(8,128)(2,1)} %param.14) | copy-start | bytes 4718596
  83.4 157.0 %copy-start.26 = (bf16[1024,768]{1,0:T(8,128)(2,1)S(1)}, bf16[1024,768]{1,0:T(8,128)(2,1)}, u32[]{:S(2)}) copy-start(bf16[1024,768]{1,0:T(8,128)(2,1)} %param.15) | copy-start | bytes 4718596
  154.3 136.9 %copy-start.61 = (f32[768]{0:T(1024)}, f32[768]{0:T(1024)S(1)}, u32[]{:S(2)}) copy-start(f32[768]{0:T(1024)S(1)} %get-tuple-element.109) | copy-start | bytes 9220
  156.2 5.2 collective-permute-start.1
  161.5 8.5 %collective-permute-start.2 = (bf16[2,96]{1,0:T(2,128)(2,1)S(1)}, bf16[2,96]{1,0:T(2,128)(2,1)S(1)}, u32[]{:S(2)}, u32[]{:S(2)}) collective-permute-start(bf16[2,96]{1,0:T(2,128)(2,1)S(1)} %pad_maximum_fusion.6), channel_id=1, source_target_pairs={{0,28},{1,29},{2,30},{3,31},{4,0},{5,1},{6,2},{7,3},{8,4},{9,5},{1... | collective-permute-start | bytes 1160 | tf_op jit(solution)/shard_map/ppermute | solution.py:23
  170.0 65.8 %collective-permute-start.3 = (bf16[2,192]{1,0:T(2,128)(2,1)S(1)}, bf16[2,192]{1,0:T(2,128)(2,1)S(1)}, u32[]{:S(2)}, u32[]{:S(2)}) collective-permute-start(bf16[2,192]{1,0:T(2,128)(2,1)S(1)} %pad_maximum_fusion.4), channel_id=1, source_target_pairs={{0,24},{1,25},{2,26},{3,27},{4,28},{5,29},{6,30},{7,31},{8,0},{9,1... | collective-permute-start | bytes 2312 | tf_op jit(solution)/shard_map/ppermute | solution.py:23
  235.8 6.2 %collective-permute-start.4 = (bf16[2,384]{1,0:T(2,128)(2,1)S(1)}, bf16[2,384]{1,0:T(2,128)(2,1)S(1)}, u32[]{:S(2)}, u32[]{:S(2)}) collective-permute-start(bf16[2,384]{1,0:T(2,128)(2,1)S(1)} %concatenate.73), channel_id=1, source_target_pairs={{0,16},{1,17},{2,18},{3,19},{4,20},{5,21},{6,22},{7,23},{8,24},{9,... | collective-permute-start | bytes 4616 | tf_op jit(solution)/shard_map/ppermute | solution.py:23
  259.9 5.0 copy-start.28
  260.1 4.8 copy-start.30
  260.3 4.6 copy-start.82
  260.7 4.7 copy-start.27
  269.1 5.6 copy-start.2
  274.2 6.3 %copy-start = (f32[12,512,512]{1,2,0:T(8,128)}, f32[12,512,512]{1,2,0:T(8,128)S(1)}, u32[]{:S(2)}) copy-start(f32[12,512,512]{1,2,0:T(8,128)S(1)} %get-tuple-element.132) | copy-start | bytes 37748740
  274.7 4.0 copy-start.64
  280.5 4.0 copy-start.56
  288.7 81.4 %copy-start.45 = (f32[1024]{0:T(1024)}, f32[1024]{0:T(1024)S(1)}, u32[]{:S(2)}) copy-start(f32[1024]{0:T(1024)S(1)} %broadcast_multiply_fusion.6) | copy-start | bytes 12292
  289.4 3.9 copy-start.52
  293.3 7.5 %copy-start.48 = (bf16[1024,8]{0,1:T(8,128)(2,1)}, bf16[1024,8]{0,1:T(8,128)(2,1)S(1)}, u32[]{:S(2)}) copy-start(bf16[1024,8]{0,1:T(8,128)(2,1)S(1)} %convolution_convert_fusion.6) | copy-start | bytes 49156
  300.8 9.6 %copy-start.47 = (bf16[3072,8]{0,1:T(8,128)(2,1)S(1)}, bf16[3072,8]{0,1:T(8,128)(2,1)}, u32[]{:S(2)}) copy-start(bf16[3072,8]{0,1:T(8,128)(2,1)} %reshape.754) | copy-start | bytes 147460
  312.1 8.9 %copy-start.50 = (bf16[1024,8]{0,1:T(8,128)(2,1)}, bf16[1024,8]{0,1:T(8,128)(2,1)S(1)}, u32[]{:S(2)}) copy-start(bf16[1024,8]{0,1:T(8,128)(2,1)S(1)} %convolution_convert_fusion.5) | copy-start | bytes 49156
  312.1 8.9 %copy-start.53 = (f32[1024]{0:T(1024)S(1)}, f32[1024]{0:T(1024)}, u32[]{:S(2)}) copy-start(f32[1024]{0:T(1024)} %copy-done.52) | copy-start | bytes 12292
  312.1 8.9 %copy-start.62 = (f32[768]{0:T(1024)S(1)}, f32[768]{0:T(1024)}, u32[]{:S(2)}) copy-start(f32[768]{0:T(1024)} %copy-done.61) | copy-start | bytes 9220
  312.1 8.9 %copy-start.69 = (f32[768]{0:T(1024)S(1)}, f32[768]{0:T(1024)}, u32[]{:S(2)}) copy-start(f32[768]{0:T(1024)} %get-tuple-element.111) | copy-start | bytes 9220
  322.1 3.5 copy-start.1
  322.5 3.0 copy-start.76
  324.7 3.5 slice-start.5
  328.2 8.1 %copy-start.18 = (bf16[1024,768]{0,1:T(8,128)(2,1)}, bf16[1024,768]{0,1:T(8,128)(2,1)S(1)}, u32[]{:S(2)}) copy-start(bf16[1024,768]{0,1:T(8,128)(2,1)S(1)} %get-tuple-element.118) | copy-start | bytes 4718596
  370.2 4.0 copy-start.80
  389.0 3.5 copy-start.14
  389.0 3.5 copy-start.42
  389.0 3.7 copy-start.31
  390.7 3.1 copy-start.29
  390.7 4.2 copy-start.12
  390.7 4.2 copy-start.55
  394.9 6.4 %copy-start.3 = (f32[12,256,256]{1,2,0:T(8,128)S(1)}, f32[12,256,256]{1,2,0:T(8,128)}, u32[]{:S(2)}) copy-start(f32[12,256,256]{1,2,0:T(8,128)} %copy-done.2) | copy-start | bytes 9437188
  394.9 6.4 %copy-start.22 = (bf16[256,768]{0,1:T(8,128)(2,1)S(1)}, bf16[256,768]{0,1:T(8,128)(2,1)}, u32[]{:S(2)}) copy-start(bf16[256,768]{0,1:T(8,128)(2,1)} %slice.306) | copy-start | bytes 1179652
  401.3 8.8 %slice-start = ((s8[12582912]{0:T(1024)(128)(4,1)}), s8[4194304]{0:T(1024)(128)(4,1)S(1)}, s32[]{:S(2)}) async-start(s8[12582912]{0:T(1024)(128)(4,1)} %bitcast.232), calls=%async_computation.5 | async-start | bytes 8388608
  402.7 7.4 %slice-start.1 = ((s8[12582912]{0:T(1024)(128)(4,1)}), s8[4194304]{0:T(1024)(128)(4,1)S(1)}, s32[]{:S(2)}) async-start(s8[12582912]{0:T(1024)(128)(4,1)} %bitcast.232), calls=%async_computation.6 | async-start | bytes 8388608
  404.6 5.5 slice-start.2
  405.3 4.8 copy-start.15
  405.3 4.8 copy-start.39
  434.5 10.7 %copy-start.33 = (bf16[128,12,64]{0,2,1:T(8,128)(2,1)S(1)}, bf16[128,12,64]{0,2,1:T(8,128)(2,1)}, u32[]{:S(2)}) copy-start(bf16[128,12,64]{0,2,1:T(8,128)(2,1)} %fusion.66) | copy-start | bytes 589828
  447.7 7.7 %slice-start.3 = ((s8[6291456]{0:T(1024)(128)(4,1)}), s8[2097152]{0:T(1024)(128)(4,1)S(1)}, s32[]{:S(2)}) async-start(s8[6291456]{0:T(1024)(128)(4,1)} %bitcast.250), calls=%async_computation.8 | async-start | bytes 4194304
  448.2 6.0 copy-start.7
  448.2 5.0 copy-start.41
  448.3 7.1 %slice-start.4 = ((s8[6291456]{0:T(1024)(128)(4,1)}), s8[4194304]{0:T(1024)(128)(4,1)S(1)}, s32[]{:S(2)}) async-start(s8[6291456]{0:T(1024)(128)(4,1)} %bitcast.250), calls=%async_computation.9 | async-start | bytes 8388608
  458.0 6.9 %copy-start.4 = (f32[1024,768]{0,1:T(8,128)S(1)}, f32[1024,768]{0,1:T(8,128)}, u32[]{:S(2)}) copy-start(f32[1024,768]{0,1:T(8,128)} %get-tuple-element.139) | copy-start | bytes 9437188
  458.0 6.9 %copy-start.46 = (f32[1024]{0:T(1024)S(1)}, f32[1024]{0:T(1024)}, u32[]{:S(2)}) copy-start(f32[1024]{0:T(1024)} %copy-done.45) | copy-start | bytes 12292
  458.1 6.9 %copy-start.54 = (f32[1024]{0:T(1024)S(1)}, f32[1024]{0:T(1024)}, u32[]{:S(2)}) copy-start(f32[1024]{0:T(1024)} %copy-done.52) | copy-start | bytes 12292
  458.1 6.9 %copy-start.71 = (f32[1024]{0:T(1024)S(1)}, f32[1024]{0:T(1024)}, u32[]{:S(2)}) copy-start(f32[1024]{0:T(1024)} %copy-done.70) | copy-start | bytes 12292
  458.1 6.9 %copy-start.73 = (f32[1024]{0:T(1024)S(1)}, f32[1024]{0:T(1024)}, u32[]{:S(2)}) copy-start(f32[1024]{0:T(1024)} %copy-done.72) | copy-start | bytes 12292
  467.3 129.8 %copy-start.32 = (f32[8,6912]{1,0:T(8,128)S(1)}, f32[8,6912]{1,0:T(8,128)}, u32[]{:S(2)}) copy-start(f32[8,6912]{1,0:T(8,128)} %param.25) | copy-start | bytes 663556
  467.3 129.9 %copy-start.43 = (f32[8,6912]{1,0:T(8,128)S(1)}, f32[8,6912]{1,0:T(8,128)}, u32[]{:S(2)}) copy-start(f32[8,6912]{1,0:T(8,128)} %param.27) | copy-start | bytes 663556
  467.3 129.9 %copy-start.44 = (f32[8,6912]{1,0:T(8,128)S(1)}, f32[8,6912]{1,0:T(8,128)}, u32[]{:S(2)}) copy-start(f32[8,6912]{1,0:T(8,128)} %param.26) | copy-start | bytes 663556
  (37 other events, 73.7 us)
Sparse Core Ops, SparseCore 0:
  11.4 60.8 all-gather.6
  75.2 52.6 all-gather.8
  131.4 63.4 all-gather.10
  198.2 61.8 all-gather.12
  458.2 136.6 all-reduce.1
